TPU v7x, 32 devices: a whole 2x2x4 slice. The times are simulated.
32 devices in a mesh: row: 4 (over x, core), col: 8 (over z, y).
Axes of the slice: x: 2, y: 2, z: 4, core: 2. Of those that a mesh axis runs over, the one named last changes fastest.
Arguments:
- rhs: float32 [32, 262144], P(None, ('row', 'col')), may hold values from -12.5 to 12.5
- near_blocks: bfloat16 [4096, 4, 4096], P(('row', 'col')), may hold values from -0.1875 to 0.1875
- near_offsets: int32 [4096, 4], P(('row', 'col')), may hold values from -4 to 4, as said below
- v_factor: bfloat16 [4096, 2048], P(('row', 'col')), may hold values from -0.75 to 0.75
- mix_col: bfloat16 [4, 128, 256, 256], P('row', 'col'), may hold values from -0.375 to 0.375
- mix_row: bfloat16 [16, 64, 128, 128], P('row', 'col'), may hold values from -0.5 to 0.5
- u_factor: bfloat16 [4096, 2048], P(('row', 'col')), may hold values from -0.75 to 0.75
Outputs:
- solution: float32 [32, 262144], P(None, ('row', 'col'))
- residual: float32 [32, 262144], P(None, ('row', 'col'))
Inputs may be any that keep to these rules, and one draw needn't show every extreme that they name: `near_offsets`: column 0 is 0; the other entries of a row are distinct and nonzero. In every aligned block of 128 rows some row holds -4 and some row holds 4.
All inputs are finite; a program needn't handle non-finite values.
Results may differ from a plain program's by a relative error of at most 0.0054.
Values may be sent and summed in bfloat16 or wider, within the bound.
A program may use at most 128 MiB of HBM per device.

v0:
```python
import jax
import jax.numpy as jnp
from jax import lax
from jax.experimental import pallas as pl
from jax.experimental.pallas import tpu as pltpu
from jax.sharding import PartitionSpec as P

LEAF = 64
RANK = 32
HALO = 4
LANES = 128
QUAD = LANES // RANK
BF16 = jnp.bfloat16
F32 = jnp.float32
MESH = pl.DeviceIdType.MESH


def iota(shape, dim):
    return lax.broadcasted_iota(jnp.int32, shape, dim)


def dot(a, b):
    return jnp.dot(a, b, preferred_element_type=F32)


def lanes_at(index, width):
    return pl.ds(pl.multiple_of(index * width, width), width)


def regroup(tiles, group):
    out = []
    for j in range(QUAD):
        made = None
        for c in range(QUAD):
            shift = (c - j) * RANK % LANES
            moved = pltpu.roll(tiles[c], shift, 1) if shift else tiles[c]
            made = moved if made is None else jnp.where(group == c, moved, made)
        out.append(made)
    return out


def kernel(
    offs, rhs_h, near_h, v_h, mixc_h, mixr_h, u_h, sol, res,
    rhs, near_raw, v_raw, mixc, mixr, u_raw,
    near_w, v_big, u_big, pick_near, pick_v, pick_u,
    xbf, xdup, w_one, w_two, q_two,
    zbuf, zrecv, tbuf, trecv, halo, part, sum_c, sum_r,
    load_sem, halo_s, halo_r, z_s, z_r, t_s, t_r, c_s, c_r, r_s, r_r,
):
    n_row = lax.axis_size("row")
    n_col = lax.axis_size("col")
    total = n_row * n_col
    row = lax.axis_index("row")
    col = lax.axis_index("col")
    me = row * n_col + col
    count, width = rhs.shape
    leaves = width // LEAF
    nnear = offs.shape[1]
    slots = leaves // n_col
    sub = slots // n_row
    edge = HALO * LEAF

    loads = {}
    for at, (name, src, dst) in enumerate(
        (("v", v_h, v_raw), ("rhs", rhs_h, rhs), ("near", near_h, near_raw),
         ("mixc", mixc_h, mixc), ("mixr", mixr_h, mixr), ("u", u_h, u_raw))
    ):
        loads[name] = pltpu.make_async_copy(src, dst, load_sem.at[at])
        loads[name].start()

    barrier = pltpu.get_barrier_semaphore()
    before = lax.rem(me + total - 1, total)
    after = lax.rem(me + 1, total)
    before_id = (before // n_col, lax.rem(before, n_col))
    after_id = (after // n_col, lax.rem(after, n_col))

    def col_id(step):
        return (row, lax.rem(col + step, n_col))

    def row_id(step):
        return (lax.rem(row + step, n_row), col)

    for step in range(1, n_col):
        pl.semaphore_signal(barrier, inc=1, device_id=col_id(step), device_id_type=MESH)
    for step in range(1, n_row):
        pl.semaphore_signal(barrier, inc=1, device_id=row_id(step), device_id_type=MESH)
    pl.semaphore_signal(barrier, inc=1, device_id=before_id, device_id_type=MESH)
    pl.semaphore_signal(barrier, inc=1, device_id=after_id, device_id_type=MESH)

    lane = iota((count, LANES), 1)
    low = lane < LEAF
    group = lane // RANK

    r = iota(pick_v.shape, 0)
    c = iota(pick_v.shape, 1)
    pick_v[...] = jnp.where((c % 16 == r // LEAF) & (c // 16 == r % LEAF // QUAD), 1.0, 0.0).astype(BF16)
    r = iota(pick_u.shape, 0)
    c = iota(pick_u.shape, 1)
    pick_u[...] = jnp.where((c % 16 == r // RANK) & (c // 16 == r % RANK // 2), 1.0, 0.0).astype(BF16)
    r = iota(pick_near.shape, 0)
    c = iota(pick_near.shape, 1)
    pick_near[...] = jnp.where((c % nnear == r // LEAF) & (c // nnear == r % LEAF // 2), 1.0, 0.0).astype(BF16)

    def prepare_v():
        loads["v"].wait()
        rr = iota((QUAD * LEAF, LANES), 0)
        gg = iota((QUAD * LEAF, LANES), 1) // RANK
        own = gg == rr % QUAD
        place = gg == rr // LEAF

        def block(b, carry):
            base = pl.multiple_of(b * 16, 16)
            rows = jnp.concatenate(
                [v_raw[pl.ds(base, 16), t * LANES:(t + 1) * LANES] for t in range(16)], axis=0
            )
            for q in range(4):
                size = QUAD * LEAF
                m = dot(pick_v[q * size:(q + 1) * size, :], rows)
                m = jnp.where(own, m, 0.0)
                m = m + pltpu.roll(m, RANK, 1)
                m = m + pltpu.roll(m, 2 * RANK, 1)
                at = pl.multiple_of(b * 16 * LEAF + q * size, size)
                v_big[pl.ds(at, size), :] = jnp.where(place, m, 0.0).astype(BF16)
            return carry

        lax.fori_loop(0, leaves // 16, block, 0)

    def prepare_u():
        loads["u"].wait()
        size = QUAD * RANK
        rr = iota((size, LANES), 0)
        half = iota((size, LANES), 1) // LEAF
        own = half == rr % 2
        place = (rr // RANK) - half

        def block(b, carry):
            base = pl.multiple_of(b * 16, 16)
            rows = jnp.concatenate(
                [u_raw[pl.ds(base, 16), t * LANES:(t + 1) * LANES] for t in range(16)], axis=0
            )
            for q in range(4):
                m = dot(pick_u[q * size:(q + 1) * size, :], rows)
                m = jnp.where(own, m, 0.0)
                m = m + pltpu.roll(m, LEAF, 1)
                at = pl.multiple_of(b * 16 * RANK + q * size, size)
                u_big[pl.ds(at, size), 0:LANES] = jnp.where(place == 0, m, 0.0).astype(BF16)
                u_big[pl.ds(at, size), LANES:2 * LANES] = jnp.where(place == 2, m, 0.0).astype(BF16)
            return carry

        lax.fori_loop(0, leaves // 16, block, 0)

    def prepare_near():
        loads["near"].wait()
        rr = iota((LEAF, LANES), 0)
        left = iota((LEAF, LANES), 1) < LEAF
        own = left == (rr % 2 == 0)
        size = nnear * LEAF // 2

        def block(b, carry):
            for k in range(2):
                leaf = b * 2 + k
                m = dot(pick_near[...], near_raw[lanes_at(leaf, size), :])
                for pair in range(nnear // 2):
                    a = jnp.where(own, m[2 * pair * LEAF:(2 * pair + 1) * LEAF], 0.0)
                    d = jnp.where(own, m[(2 * pair + 1) * LEAF:(2 * pair + 2) * LEAF], 0.0)
                    made = jnp.where(left, a, d) + pltpu.roll(jnp.where(left, d, a), LEAF, 1)
                    near_w[lanes_at(leaf, LEAF), pair * LANES:(pair + 1) * LANES] = made.astype(BF16)
            return carry

        lax.fori_loop(0, leaves // 2, block, 0)

    def spread(tile, first):
        turned = pltpu.roll(tile, LEAF, 1)
        xdup[first] = jnp.where(low, tile, turned).astype(BF16)
        xdup[first + 1] = jnp.where(low, turned, tile).astype(BF16)

    def remote(src, dst, send, recv, to):
        return pltpu.make_async_remote_copy(
            src_ref=src, dst_ref=dst, send_sem=send, recv_sem=recv, device_id=to, device_id_type=MESH
        )

    def all_sum(at, rows):
        eye = iota((count, LANES), 0) == lane
        pick = iota((8, LANES), 0)
        tile = jnp.zeros((8, LANES), F32)
        for k, acc in enumerate(rows):
            line = jnp.sum(jnp.where(eye, jnp.sum(acc, axis=1, keepdims=True), 0.0), axis=0, keepdims=True)
            tile = jnp.where(pick == k, line, tile)
        for slot, n, here, buf, send, recv, ids in (
            (0, n_col, col, sum_c, c_s, c_r, col_id), (1, n_row, row, sum_r, r_s, r_r, row_id)
        ):
            part[at, slot] = tile
            buf[at, 0] = tile
            copies = [
                remote(part.at[at, slot], buf.at[at, s], send.at[at, s], recv.at[at, s], ids(s))
                for s in range(1, n)
            ]
            for copy in copies:
                copy.start()
            for copy in copies:
                copy.wait()
            tile = buf[at, here]
            for source in range(1, n):
                tile = tile + buf[at, lax.rem(here + n - source, n)]
        return [
            jnp.sum(jnp.where(eye, tile[k:k + 1, :], 0.0), axis=1, keepdims=True) for k in range(len(rows))
        ]

    def operator(at, x, w, others):
        h_low = remote(xbf.at[:, width - edge:width], halo.at[at, 0], halo_s.at[at, 0], halo_r.at[at, 0], after_id)
        h_high = remote(xbf.at[:, 0:edge], halo.at[at, 1], halo_s.at[at, 1], halo_r.at[at, 1], before_id)
        h_low.start()
        h_high.start()
        tiles = slots // QUAD
        for g4 in range(leaves // QUAD):
            z = dot(xbf[:, g4 * 256:(g4 + 1) * 256], v_big[g4 * 256:(g4 + 1) * 256, :])
            zbuf[g4 // tiles, :, g4 % tiles * LANES:(g4 % tiles + 1) * LANES] = z.astype(BF16)
        z_copies = []
        for s in range(1, n_col):
            z_copies.append(
                remote(zbuf.at[lax.rem(col + s, n_col)], zrecv.at[at, s], z_s.at[at, s], z_r.at[at, s], col_id(s))
            )
            z_copies[-1].start()
        zrecv[at, 0] = zbuf[col]
        if at == 0:
            prepare_near()
        h_low.wait()
        h_high.wait()
        for side, beyond, first in ((0, me == 0, 0), (1, me == total - 1, leaves + HALO)):
            for k in range(HALO // 2):
                tile = halo[at, side, :, k * LANES:(k + 1) * LANES].astype(F32)
                spread(jnp.where(beyond, 0.0, tile), first + 2 * k)

        def near(b, carry):
            for pair in range(4):
                outs = []
                for k in range(2):
                    leaf = b * 8 + pair * 2 + k
                    picked = [xdup[leaf + HALO + offs[leaf, n]] for n in range(nnear)]
                    left = jnp.concatenate(
                        [jnp.where(low, picked[2 * m], picked[2 * m + 1]) for m in range(nnear // 2)], axis=1
                    )
                    outs.append(
                        lax.dot_general(
                            left, near_w[lanes_at(leaf, LEAF), :], (((1,), (1,)), ((), ())),
                            preferred_element_type=F32,
                        )
                    )
                where = lanes_at(b * 4 + pair, LANES)
                w[:, where] = x[:, where] + jnp.concatenate(outs, axis=1)
            return carry

        steps = leaves // 8
        lax.fori_loop(0, steps // 2, near, 0)
        for copy in z_copies:
            copy.wait()
        if at == 0:
            loads["mixc"].wait()
        for jt in range(tiles):
            lefts = [[] for _ in range(QUAD)]
            for cq in range(n_col // QUAD):
                got = regroup(
                    [
                        zrecv[at, lax.rem(col + n_col - (cq * QUAD + c4), n_col), :, jt * LANES:(jt + 1) * LANES].astype(F32)
                        for c4 in range(QUAD)
                    ],
                    group,
                )
                for j4 in range(QUAD):
                    lefts[j4].append(got[j4].astype(BF16))
            for j4 in range(QUAD):
                j = jt * QUAD + j4
                first = dot(jnp.concatenate(lefts[j4], axis=1), mixc[j])
                tbuf[j // sub, j % sub] = first.astype(BF16)
        t_copies = []
        for s in range(1, n_row):
            t_copies.append(
                remote(tbuf.at[lax.rem(row + s, n_row)], trecv.at[at, s], t_s.at[at, s], t_r.at[at, s], row_id(s))
            )
            t_copies[-1].start()
        trecv[at, 0] = tbuf[row]
        if at == 0:
            prepare_u()
        lax.fori_loop(steps // 2, steps, near, 0)
        for copy in t_copies:
            copy.wait()
        if at == 0:
            loads["mixr"].wait()
        sums = [jnp.zeros((count, LANES), F32) for _ in range(len(others) + 1)]
        for i in range(sub):
            for pq in range(n_col // QUAD):
                lefts = [[] for _ in range(QUAD)]
                for rq in range(n_row // QUAD):
                    got = regroup(
                        [
                            trecv[at, lax.rem(row + n_row - (rq * QUAD + r4), n_row), i, :, pq * LANES:(pq + 1) * LANES].astype(F32)
                            for r4 in range(QUAD)
                        ],
                        group,
                    )
                    for p4 in range(QUAD):
                        lefts[p4].append(got[p4].astype(BF16))
                for p4 in range(QUAD):
                    p = pq * QUAD + p4
                    second = dot(jnp.concatenate(lefts[p4], axis=1), mixr[i, p]).astype(BF16)
                    for tt in range(n_row // QUAD):
                        at4 = (i * n_col + p) * (n_row // QUAD) + tt
                        far = dot(second[:, tt * LANES:(tt + 1) * LANES], u_big[at4 * LANES:(at4 + 1) * LANES, :])
                        for k in range(2):
                            where = slice(at4 * 256 + k * LANES, at4 * 256 + (k + 1) * LANES)
                            image = w[:, where] + far[:, k * LANES:(k + 1) * LANES]
                            w[:, where] = image
                            for m, other in enumerate(others):
                                sums[m] = sums[m] + other[:, where] * image
                            sums[-1] = sums[-1] + image * image
        return sums

    prepare_v()
    loads["rhs"].wait()

    def start_tile(t, acc):
        where = lanes_at(t, LANES)
        tile = rhs[:, where]
        xbf[:, where] = tile.astype(BF16)
        spread(tile, HALO + 2 * t)
        return acc + tile * tile

    norm = lax.fori_loop(0, width // LANES, start_tile, jnp.zeros((count, LANES), F32))
    pl.semaphore_wait(barrier, n_col + n_row)
    first = operator(0, rhs, w_one, (rhs,))
    norm_sq, cross, image_sq = all_sum(0, [norm] + first)
    beta = jnp.sqrt(norm_sq)
    h11 = cross / norm_sq
    h21 = jnp.sqrt(image_sq / norm_sq - h11 * h11)
    scale = 1.0 / (beta * h21)

    def second_tile(t, carry):
        where = lanes_at(t, LANES)
        tile = (w_one[:, where] - h11 * rhs[:, where]) * scale
        q_two[:, where] = tile
        xbf[:, where] = tile.astype(BF16)
        spread(tile, HALO + 2 * t)
        return carry

    lax.fori_loop(0, width // LANES, second_tile, 0)
    second = operator(1, q_two, w_two, (rhs, q_two))
    with_first, h22, image_sq = all_sum(1, second)
    h12 = with_first / beta
    h32 = jnp.sqrt(image_sq - (h12 * h12 + h22 * h22))
    m11 = h11 * h11 + h21 * h21
    m12 = h11 * h12 + h21 * h22
    m22 = h12 * h12 + h22 * h22 + h32 * h32
    det = m11 * m22 - m12 * m12
    y1 = (m22 * h11 - m12 * h12) / det
    y2 = beta * (m11 * h12 - m12 * h11) / det

    def last_tile(t, carry):
        where = lanes_at(t, LANES)
        sol[:, where] = y1 * rhs[:, where] + y2 * q_two[:, where]
        res[:, where] = rhs[:, where] - y1 * w_one[:, where] - y2 * w_two[:, where]
        return carry

    lax.fori_loop(0, width // LANES, last_tile, 0)


def body(rhs, near_blocks, near_offsets, v_factor, mix_col, mix_row, u_factor):
    n_row = lax.axis_size("row")
    n_col = lax.axis_size("col")
    count, width = rhs.shape
    leaves, nnear = near_offsets.shape
    pieces = near_blocks.shape[2] // LANES
    near_rows = (
        near_blocks.reshape(leaves, nnear, pieces, LANES).transpose(0, 2, 1, 3).reshape(leaves * pieces * nnear, LANES)
    )
    mixc = mix_col[0]
    slots = leaves // n_col
    sub = slots // n_row
    vmem = pltpu.VMEM
    dma = pltpu.SemaphoreType.DMA
    field = vmem((count, width), F32)
    any_spec = pl.BlockSpec(memory_space=pl.ANY)
    return pl.pallas_call(
        kernel,
        out_shape=(jax.ShapeDtypeStruct((count, width), F32),) * 2,
        in_specs=[pl.BlockSpec(memory_space=pltpu.SMEM)] + [any_spec] * 6,
        out_specs=(pl.BlockSpec(memory_space=pltpu.VMEM),) * 2,
        scratch_shapes=[
            field,
            vmem(near_rows.shape, BF16),
            vmem(v_factor.shape, BF16),
            vmem(mixc.shape, BF16),
            vmem(mix_row.shape, BF16),
            vmem(u_factor.shape, BF16),
            vmem((leaves * LEAF, nnear * LEAF), BF16),
            vmem((leaves * LEAF, LANES), BF16),
            vmem((leaves * RANK, 2 * LANES), BF16),
            vmem((nnear * LEAF, pieces * nnear), BF16),
            vmem((16 * LEAF, 256), BF16),
            vmem((16 * RANK, 256), BF16),
            vmem((count, width), BF16),
            vmem((leaves + 2 * HALO, count, LANES), BF16),
            field,
            field,
            field,
            vmem((n_col, count, slots * RANK), BF16),
            vmem((2, n_col, count, slots * RANK), BF16),
            vmem((n_row, sub, count, n_col * RANK), BF16),
            vmem((2, n_row, sub, count, n_col * RANK), BF16),
            vmem((2, 2, count, HALO * LEAF), BF16),
            vmem((2, 2, 8, LANES), F32),
            vmem((2, n_col, 8, LANES), F32),
            vmem((2, n_row, 8, LANES), F32),
            dma((6,)),
            dma((2, 2)),
            dma((2, 2)),
            dma((2, n_col)),
            dma((2, n_col)),
            dma((2, n_row)),
            dma((2, n_row)),
            dma((2, n_col)),
            dma((2, n_col)),
            dma((2, n_row)),
            dma((2, n_row)),
        ],
        compiler_params=pltpu.CompilerParams(
            collective_id=0, has_side_effects=True, vmem_limit_bytes=60 * 1024 * 1024
        ),
        name="gmres",
    )(near_offsets, rhs, near_rows, v_factor, mixc, mix_row, u_factor)


def solution(mesh):
    in_specs = (
        P(None, ("row", "col")),
        P(("row", "col"), None, None),
        P(("row", "col"), None),
        P(("row", "col"), None),
        P("row", "col", None, None),
        P("row", "col", None, None),
        P(("row", "col"), None),
    )
    out_specs = (P(None, ("row", "col")), P(None, ("row", "col")))
    return jax.shard_map(body, mesh=mesh, in_specs=in_specs, out_specs=out_specs, check_vma=False)
```

profile of v0, /device:TPU:0, one launch (start us, length us, event | category | flops | bytes accessed | tf_op | source)
XLA Modules:
  0.0 82.8 jit_solution(17462489444094387649)
XLA Ops:
  0.6 1.4 %copy.10.offs = s32[128,4]{1,0:T(8,128)} copy(s32[128,4]{0,1:T(4,128)} %param.9) | data formatting | bytes 4096 | tf_op args[2]
  2.0 76.2 %gmres.1 = (f32[32,8192]{1,0:T(8,128)}, f32[32,8192]{1,0:T(8,128)}) custom-call(s32[128,4]{1,0:T(8,128)} %copy.10.offs, f32[32,8192]{1,0:T(8,128)} %rhs_h.1, bf16[16384,128]{1,0:T(8,128)(2,1)} %bitcast.6, bf16[128,2048]{1,0:T(8,128)(2,1)} %v_h.1, bf16[16,256,256]{2,1,0:T(8,128)(2,1)} %bitcast.7, bf16[4,8,128,128]{3,2,1,0:T(8,128)(2,1)} %mixr_h.1, ...), custom_call_target="tpu_custom_call" | custom-call | tf_op jit(solution)/shard_map/gmres/pallas_call | solution.py:382
  78.2 2.3 %copy.13 = f32[32,8192]{1,0:T(8,128)} copy(f32[32,8192]{1,0:T(8,128)} %get-tuple-element.4) | data formatting | bytes 2097152
  80.5 2.3 %copy.14 = f32[32,8192]{1,0:T(8,128)} copy(f32[32,8192]{1,0:T(8,128)} %get-tuple-element.5) | data formatting | bytes 2097152
where the time goes:
time: 83.1 us; the launch traced here: 82.8 us
  Pallas kernels  76.2 us (92%)
  local copies, waits for them, and re-layouts  5.94 us (7%)
    pallas_call x1, Pallas kernels, body(): pl.pallas_call(kernel, out_shape=(jax.ShapeDtypeStruct((count, width), F3...  76.2 us
    unnamed x3, local copies, waits for them, and re-layouts  5.94 us

commit v1 on v0

--- a/solution.py
+++ b/solution.py
@@ -44,8 +44,8 @@
     rhs, near_raw, v_raw, mixc, mixr, u_raw,
     near_w, v_big, u_big, pick_near, pick_v, pick_u,
     xbf, xdup, w_one, w_two, q_two,
-    zbuf, zrecv, tbuf, trecv, halo, part, sum_c, sum_r,
-    load_sem, halo_s, halo_r, z_s, z_r, t_s, t_r, c_s, c_r, r_s, r_r,
+    zbuf, zrecv, tbuf, trecv, halo, part, sums,
+    load_sem, halo_s, halo_r, z_s, z_r, t_s, t_r, sum_s, sum_r,
 ):
     n_row = lax.axis_size("row")
     n_col = lax.axis_size("col")
@@ -66,7 +66,8 @@
          ("mixc", mixc_h, mixc), ("mixr", mixr_h, mixr), ("u", u_h, u_raw))
     ):
         loads[name] = pltpu.make_async_copy(src, dst, load_sem.at[at])
-        loads[name].start()
+        if name in ("v", "rhs"):
+            loads[name].start()
 
     barrier = pltpu.get_barrier_semaphore()
     before = lax.rem(me + total - 1, total)
@@ -80,12 +81,15 @@
     def row_id(step):
         return (lax.rem(row + step, n_row), col)
 
-    for step in range(1, n_col):
-        pl.semaphore_signal(barrier, inc=1, device_id=col_id(step), device_id_type=MESH)
-    for step in range(1, n_row):
-        pl.semaphore_signal(barrier, inc=1, device_id=row_id(step), device_id_type=MESH)
-    pl.semaphore_signal(barrier, inc=1, device_id=before_id, device_id_type=MESH)
-    pl.semaphore_signal(barrier, inc=1, device_id=after_id, device_id_type=MESH)
+    def any_id(step):
+        other = lax.rem(me + step, total)
+        return (other // n_col, lax.rem(other, n_col))
+
+    def greet(step, carry):
+        pl.semaphore_signal(barrier, inc=1, device_id=any_id(step), device_id_type=MESH)
+        return carry
+
+    lax.fori_loop(1, total, greet, 0)
 
     lane = iota((count, LANES), 1)
     low = lane < LEAF
@@ -103,6 +107,8 @@
 
     def prepare_v():
         loads["v"].wait()
+        for name in ("near", "mixc", "mixr", "u"):
+            loads[name].start()
         rr = iota((QUAD * LEAF, LANES), 0)
         gg = iota((QUAD * LEAF, LANES), 1) // RANK
         own = gg == rr % QUAD
@@ -158,16 +164,25 @@
 
         def block(b, carry):
             for k in range(2):
-                leaf = b * 2 + k
-                m = dot(pick_near[...], near_raw[lanes_at(leaf, size), :])
-                for pair in range(nnear // 2):
-                    a = jnp.where(own, m[2 * pair * LEAF:(2 * pair + 1) * LEAF], 0.0)
-                    d = jnp.where(own, m[(2 * pair + 1) * LEAF:(2 * pair + 2) * LEAF], 0.0)
-                    made = jnp.where(left, a, d) + pltpu.roll(jnp.where(left, d, a), LEAF, 1)
-                    near_w[lanes_at(leaf, LEAF), pair * LANES:(pair + 1) * LANES] = made.astype(BF16)
-            return carry
-
-        lax.fori_loop(0, leaves // 2, block, 0)
+                twin = b * 4 + k * 2
+                both = dot(
+                    pick_near[...],
+                    jnp.concatenate(
+                        [near_raw[lanes_at(twin, size), :], near_raw[lanes_at(twin + 1, size), :]], axis=1
+                    ),
+                )
+                for which in range(2):
+                    m = both[:, which * LANES:(which + 1) * LANES]
+                    for pair in range(nnear // 2):
+                        a = m[2 * pair * LEAF:(2 * pair + 1) * LEAF]
+                        d = m[(2 * pair + 1) * LEAF:(2 * pair + 2) * LEAF]
+                        straight = jnp.where(own, jnp.where(left, a, d), 0.0)
+                        crossed = jnp.where(own, jnp.where(left, d, a), 0.0)
+                        made = straight + pltpu.roll(crossed, LEAF, 1)
+                        near_w[lanes_at(twin + which, LEAF), pair * LANES:(pair + 1) * LANES] = made.astype(BF16)
+            return carry
+
+        lax.fori_loop(0, leaves // 4, block, 0)
 
     def spread(tile, first):
         turned = pltpu.roll(tile, LEAF, 1)
@@ -180,30 +195,33 @@
         )
 
     def all_sum(at, rows):
-        eye = iota((count, LANES), 0) == lane
-        pick = iota((8, LANES), 0)
-        tile = jnp.zeros((8, LANES), F32)
+        spot = lane - iota((count, LANES), 0)
+        spread_out = jnp.zeros((count, LANES), F32)
         for k, acc in enumerate(rows):
-            line = jnp.sum(jnp.where(eye, jnp.sum(acc, axis=1, keepdims=True), 0.0), axis=0, keepdims=True)
-            tile = jnp.where(pick == k, line, tile)
-        for slot, n, here, buf, send, recv, ids in (
-            (0, n_col, col, sum_c, c_s, c_r, col_id), (1, n_row, row, sum_r, r_s, r_r, row_id)
-        ):
-            part[at, slot] = tile
-            buf[at, 0] = tile
-            copies = [
-                remote(part.at[at, slot], buf.at[at, s], send.at[at, s], recv.at[at, s], ids(s))
-                for s in range(1, n)
-            ]
-            for copy in copies:
-                copy.start()
-            for copy in copies:
-                copy.wait()
-            tile = buf[at, here]
-            for source in range(1, n):
-                tile = tile + buf[at, lax.rem(here + n - source, n)]
+            spread_out = jnp.where(spot == k * count, jnp.sum(acc, axis=1, keepdims=True), spread_out)
+        line = jnp.sum(spread_out, axis=0, keepdims=True)
+        part[at] = line
+        sums[at, 0] = line
+
+        def copy(s):
+            return remote(part.at[at], sums.at[at, s], sum_s.at[at, s], sum_r.at[at, s], any_id(s))
+
+        def start(s, carry):
+            copy(s).start()
+            return carry
+
+        def wait(s, carry):
+            copy(s).wait()
+            return carry
+
+        lax.fori_loop(1, total, start, 0)
+        lax.fori_loop(1, total, wait, 0)
+        parts = [sums[at, lax.rem(me + total - d, total)] for d in range(total)]
+        while len(parts) > 1:
+            parts = [parts[i] + parts[i + 1] for i in range(0, len(parts), 2)]
+        line = parts[0]
         return [
-            jnp.sum(jnp.where(eye, tile[k:k + 1, :], 0.0), axis=1, keepdims=True) for k in range(len(rows))
+            jnp.sum(jnp.where(spot == k * count, line, 0.0), axis=1, keepdims=True) for k in range(len(rows))
         ]
 
     def operator(at, x, w, others):
@@ -286,7 +304,7 @@
             copy.wait()
         if at == 0:
             loads["mixr"].wait()
-        sums = [jnp.zeros((count, LANES), F32) for _ in range(len(others) + 1)]
+        accs = [jnp.zeros((count, LANES), F32) for _ in range(len(others) + 1)]
         for i in range(sub):
             for pq in range(n_col // QUAD):
                 lefts = [[] for _ in range(QUAD)]
@@ -311,9 +329,9 @@
                             image = w[:, where] + far[:, k * LANES:(k + 1) * LANES]
                             w[:, where] = image
                             for m, other in enumerate(others):
-                                sums[m] = sums[m] + other[:, where] * image
-                            sums[-1] = sums[-1] + image * image
-        return sums
+                                accs[m] = accs[m] + other[:, where] * image
+                            accs[-1] = accs[-1] + image * image
+        return accs
 
     prepare_v()
     loads["rhs"].wait()
@@ -326,7 +344,7 @@
         return acc + tile * tile
 
     norm = lax.fori_loop(0, width // LANES, start_tile, jnp.zeros((count, LANES), F32))
-    pl.semaphore_wait(barrier, n_col + n_row)
+    pl.semaphore_wait(barrier, total - 1)
     first = operator(0, rhs, w_one, (rhs,))
     norm_sq, cross, image_sq = all_sum(0, [norm] + first)
     beta = jnp.sqrt(norm_sq)
@@ -375,14 +393,16 @@
     mixc = mix_col[0]
     slots = leaves // n_col
     sub = slots // n_row
+    total = n_row * n_col
+    operands = (rhs, near_rows, v_factor, mixc, mix_row, u_factor)
     vmem = pltpu.VMEM
     dma = pltpu.SemaphoreType.DMA
     field = vmem((count, width), F32)
-    any_spec = pl.BlockSpec(memory_space=pl.ANY)
+    hbm_spec = pl.BlockSpec(memory_space=pltpu.HBM)
     return pl.pallas_call(
         kernel,
         out_shape=(jax.ShapeDtypeStruct((count, width), F32),) * 2,
-        in_specs=[pl.BlockSpec(memory_space=pltpu.SMEM)] + [any_spec] * 6,
+        in_specs=[pl.BlockSpec(memory_space=pltpu.SMEM)] + [hbm_spec] * 6,
         out_specs=(pl.BlockSpec(memory_space=pltpu.VMEM),) * 2,
         scratch_shapes=[
             field,
@@ -407,9 +427,8 @@
             vmem((n_row, sub, count, n_col * RANK), BF16),
             vmem((2, n_row, sub, count, n_col * RANK), BF16),
             vmem((2, 2, count, HALO * LEAF), BF16),
-            vmem((2, 2, 8, LANES), F32),
-            vmem((2, n_col, 8, LANES), F32),
-            vmem((2, n_row, 8, LANES), F32),
+            vmem((2, 1, LANES), F32),
+            vmem((2, total, 1, LANES), F32),
             dma((6,)),
             dma((2, 2)),
             dma((2, 2)),
@@ -417,16 +436,14 @@
             dma((2, n_col)),
             dma((2, n_row)),
             dma((2, n_row)),
-            dma((2, n_col)),
-            dma((2, n_col)),
-            dma((2, n_row)),
-            dma((2, n_row)),
+            dma((2, total)),
+            dma((2, total)),
         ],
         compiler_params=pltpu.CompilerParams(
-            collective_id=0, has_side_effects=True, vmem_limit_bytes=60 * 1024 * 1024
+            collective_id=0, has_side_effects=True, vmem_limit_bytes=34 * 1024 * 1024
         ),
         name="gmres",
-    )(near_offsets, rhs, near_rows, v_factor, mixc, mix_row, u_factor)
+    )(near_offsets, *(pltpu.with_memory_space_constraint(a, pltpu.HBM) for a in operands))
 
 
 def solution(mesh):

time: 83.1 us -> 69.4 us (0.84)
  Pallas kernels: 76.2 us -> 65.8 us
  local copies, waits for them, and re-layouts: 5.94 us -> 2.73 us
    pallas_call x1, Pallas kernels: 76.2 us -> 65.8 us  [body(): pl.pallas_call(kernel, out_shape=(jax.ShapeDtypeStruct((count, width), F3...]
    unnamed x3, local copies, waits for them, and re-layouts: 5.94 us -> 2.73 us
where the time goes in v1:
time: 69.4 us; the launch traced here: 69.2 us
  Pallas kernels  65.8 us (95%)
  local copies, waits for them, and re-layouts  2.73 us (4%)
    pallas_call x1, Pallas kernels, body(): pl.pallas_call(kernel, out_shape=(jax.ShapeDtypeStruct((count, width), F3...  65.8 us
    unnamed x3, local copies, waits for them, and re-layouts  2.73 us

profile of v1, /device:TPU:0, one launch (start us, length us, event | category | flops | bytes accessed | tf_op | source)
XLA Modules:
  0.0 69.2 jit_solution(7927183173807085432)
XLA Ops:
  0.6 0.8 %copy.10.offs = s32[128,4]{1,0:T(8,128)S(1)} copy(s32[128,4]{0,1:T(4,128)} %param.9) | data formatting | bytes 4096 | tf_op args[2]
  1.4 65.8 %gmres.1 = (f32[32,8192]{1,0:T(8,128)S(1)}, f32[32,8192]{1,0:T(8,128)S(1)}) custom-call(s32[128,4]{1,0:T(8,128)S(1)} %copy.10.offs, f32[32,8192]{1,0:T(8,128)} %rhs_h.1, bf16[16384,128]{1,0:T(8,128)(2,1)} %bitcast.6, bf16[128,2048]{1,0:T(8,128)(2,1)} %v_h.1, bf16[16,256,256]{2,1,0:T(8,128)(2,1)} %bitcast.7, bf16[4,8,128,128]{3,2,1,0:T(8,128)(2,1)} %mixr_h.1, ...), custom_call_target="tpu_custom_call" | custom-call | tf_op jit(solution)/shard_map/gmres/pallas_call | solution.py:402
  67.3 1.0 %copy.13 = f32[32,8192]{1,0:T(8,128)} copy(f32[32,8192]{1,0:T(8,128)S(1)} %get-tuple-element.4) | data formatting | bytes 2097152
  68.2 1.0 %copy.14 = f32[32,8192]{1,0:T(8,128)} copy(f32[32,8192]{1,0:T(8,128)S(1)} %get-tuple-element.5) | data formatting | bytes 2097152

commit v2 on v1

--- a/solution.py
+++ b/solution.py
@@ -42,7 +42,7 @@
 def kernel(
     offs, rhs_h, near_h, v_h, mixc_h, mixr_h, u_h, sol, res,
     rhs, near_raw, v_raw, mixc, mixr, u_raw,
-    near_w, v_big, u_big, pick_near, pick_v, pick_u,
+    near_w, v_big, u_big, pick_near, pick_v, pick_u, order,
     xbf, xdup, w_one, w_two, q_two,
     zbuf, zrecv, tbuf, trecv, halo, part, sums,
     load_sem, halo_s, halo_r, z_s, z_r, t_s, t_r, sum_s, sum_r,
@@ -55,7 +55,8 @@
     me = row * n_col + col
     count, width = rhs.shape
     leaves = width // LEAF
-    nnear = offs.shape[1]
+    nnear = offs.shape[0]
+    pieces = LEAF // 2
     slots = leaves // n_col
     sub = slots // n_row
     edge = HALO * LEAF
@@ -103,7 +104,11 @@
     pick_u[...] = jnp.where((c % 16 == r // RANK) & (c // 16 == r % RANK // 2), 1.0, 0.0).astype(BF16)
     r = iota(pick_near.shape, 0)
     c = iota(pick_near.shape, 1)
-    pick_near[...] = jnp.where((c % nnear == r // LEAF) & (c // nnear == r % LEAF // 2), 1.0, 0.0).astype(BF16)
+    pick_near[...] = jnp.where((c % nnear == r // pieces) & (c // nnear == r % pieces), 1.0, 0.0).astype(BF16)
+
+    r = iota(order.shape, 0) % LANES
+    c = iota(order.shape, 1)
+    order[...] = jnp.where(c == r // LEAF * LEAF + r % pieces * 2 + r % LEAF // pieces, 1.0, 0.0).astype(BF16)
 
     def prepare_v():
         loads["v"].wait()
@@ -157,9 +162,7 @@
 
     def prepare_near():
         loads["near"].wait()
-        rr = iota((LEAF, LANES), 0)
-        left = iota((LEAF, LANES), 1) < LEAF
-        own = left == (rr % 2 == 0)
+        left = iota((pieces, LANES), 1) < LEAF
         size = nnear * LEAF // 2
 
         def block(b, carry):
@@ -174,12 +177,14 @@
                 for which in range(2):
                     m = both[:, which * LANES:(which + 1) * LANES]
                     for pair in range(nnear // 2):
-                        a = m[2 * pair * LEAF:(2 * pair + 1) * LEAF]
-                        d = m[(2 * pair + 1) * LEAF:(2 * pair + 2) * LEAF]
-                        straight = jnp.where(own, jnp.where(left, a, d), 0.0)
-                        crossed = jnp.where(own, jnp.where(left, d, a), 0.0)
-                        made = straight + pltpu.roll(crossed, LEAF, 1)
-                        near_w[lanes_at(twin + which, LEAF), pair * LANES:(pair + 1) * LANES] = made.astype(BF16)
+                        a = m[2 * pair * pieces:(2 * pair + 1) * pieces]
+                        d = m[(2 * pair + 1) * pieces:(2 * pair + 2) * pieces]
+                        even = jnp.where(left, a, pltpu.roll(d, LEAF, 1))
+                        odd = jnp.where(left, pltpu.roll(a, LEAF, 1), d)
+                        for parity, made in ((0, even), (1, odd)):
+                            near_w[
+                                lanes_at((twin + which) * 2 + parity, pieces), pair * LANES:(pair + 1) * LANES
+                            ] = made.astype(BF16)
             return carry
 
         lax.fori_loop(0, leaves // 4, block, 0)
@@ -254,7 +259,7 @@
                 outs = []
                 for k in range(2):
                     leaf = b * 8 + pair * 2 + k
-                    picked = [xdup[leaf + HALO + offs[leaf, n]] for n in range(nnear)]
+                    picked = [xdup[leaf + HALO + offs[n, leaf]] for n in range(nnear)]
                     left = jnp.concatenate(
                         [jnp.where(low, picked[2 * m], picked[2 * m + 1]) for m in range(nnear // 2)], axis=1
                     )
@@ -265,7 +270,10 @@
                         )
                     )
                 where = lanes_at(b * 4 + pair, LANES)
-                w[:, where] = x[:, where] + jnp.concatenate(outs, axis=1)
+                both = jnp.concatenate(outs, axis=1)
+                high = both.astype(BF16)
+                rest = (both - high.astype(F32)).astype(BF16)
+                w[:, where] = x[:, where] + dot(jnp.concatenate([high, rest], axis=1), order[...])
             return carry
 
         steps = leaves // 8
@@ -414,9 +422,10 @@
             vmem((leaves * LEAF, nnear * LEAF), BF16),
             vmem((leaves * LEAF, LANES), BF16),
             vmem((leaves * RANK, 2 * LANES), BF16),
-            vmem((nnear * LEAF, pieces * nnear), BF16),
+            vmem((nnear * pieces, pieces * nnear), BF16),
             vmem((16 * LEAF, 256), BF16),
             vmem((16 * RANK, 256), BF16),
+            vmem((2 * LANES, LANES), BF16),
             vmem((count, width), BF16),
             vmem((leaves + 2 * HALO, count, LANES), BF16),
             field,
@@ -443,7 +452,7 @@
             collective_id=0, has_side_effects=True, vmem_limit_bytes=34 * 1024 * 1024
         ),
         name="gmres",
-    )(near_offsets, *(pltpu.with_memory_space_constraint(a, pltpu.HBM) for a in operands))
+    )(near_offsets.T, *(pltpu.with_memory_space_constraint(a, pltpu.HBM) for a in operands))
 
 
 def solution(mesh):

time: 69.4 us -> 84 us (1.21)
  Pallas kernels: 65.8 us -> 80.6 us
    pallas_call x1, Pallas kernels: 65.8 us -> 80.6 us  [body(): pl.pallas_call(kernel, out_shape=(jax.ShapeDtypeStruct((count, width), F3...]
    unnamed x3 -> x4, local copies, waits for them, and re-layouts: 2.73 us -> 2.62 us
where the time goes in v2:
time: 84 us; the launch traced here: 83.9 us
  Pallas kernels  80.6 us (96%)
  local copies, waits for them, and re-layouts  2.62 us (3%)
    pallas_call x1, Pallas kernels, body(): pl.pallas_call(kernel, out_shape=(jax.ShapeDtypeStruct((count, width), F3...  80.6 us
    unnamed x4, local copies, waits for them, and re-layouts  2.62 us

profile of v2, /device:TPU:0, one launch (start us, length us, event | category | flops | bytes accessed | tf_op | source)
XLA Modules:
  0.0 83.9 jit_solution(16200378924741615865)
XLA Ops:
  0.6 0.0 copy-start
  0.6 0.7 copy-done
  1.3 80.6 %gmres.1 = (f32[32,8192]{1,0:T(8,128)S(1)}, f32[32,8192]{1,0:T(8,128)S(1)}) custom-call(s32[4,128]{1,0:T(4,128)S(1)} %bitcast.7, f32[32,8192]{1,0:T(8,128)} %rhs_h.1, bf16[16384,128]{1,0:T(8,128)(2,1)} %bitcast.8, bf16[128,2048]{1,0:T(8,128)(2,1)} %v_h.1, bf16[16,256,256]{2,1,0:T(8,128)(2,1)} %bitcast.9, bf16[4,8,128,128]{3,2,1,0:T(8,128)(2,1)} %mixr_h.1, ...), custom_call_target="tpu_custom_call" | custom-call | tf_op jit(solution)/shard_map/gmres/pallas_call | solution.py:410
  81.9 1.0 %copy.12 = f32[32,8192]{1,0:T(8,128)} copy(f32[32,8192]{1,0:T(8,128)S(1)} %get-tuple-element.4) | data formatting | bytes 2097152
  82.9 1.0 %copy.13 = f32[32,8192]{1,0:T(8,128)} copy(f32[32,8192]{1,0:T(8,128)S(1)} %get-tuple-element.5) | data formatting | bytes 2097152
Async XLA Ops:
  0.6 0.7 copy-start
